TPU v7x, 32 devices: a whole 2x2x4 slice. The times are simulated.
32 devices in a mesh: seq: 16 (over z, y, core), head: 2 (over x).
Axes of the slice: x: 2, y: 2, z: 4, core: 2. Of those that a mesh axis runs over, the one named last changes fastest.
Arguments:
- sequence: bfloat16 [8192, 2048], P('seq'), may hold values from -6 to 6
- input_weight: bfloat16 [2048, 4096], P(None, 'head'), may hold values from -0.125 to 0.125
- gate_weight: bfloat16 [2048, 4096], P(None, 'head'), may hold values from -0.125 to 0.125
- state_weight: bfloat16 [2048, 256], replicated, may hold values from -0.015625 to 0.015625
- step_weight: bfloat16 [2048, 64], P(None, 'head'), may hold values from -0.125 to 0.125
- step_bias: float32 [64], P('head'), may hold values from -2 to 0
- decay_rate: float32 [64], P('head'), may hold values from 6.1035156e-05 to 0.1
- skip_gain: float32 [64], P('head'), may hold values from 0.5 to 1.5
- output_weight: bfloat16 [4096, 2048], P('head'), may hold values from -0.09375 to 0.09375
Outputs:
- encoded: bfloat16 [8192, 2048], P('seq', 'head')
All inputs are finite; a program needn't handle non-finite values.
Results may differ from a plain program's by a relative error of at most 0.014.
Values sent between devices are 32-bit elements; how exact they have to be, the bound alone decides.
A program may use at most 128 MiB of HBM per device.

v0:
```python
import functools

import jax
import jax.numpy as jnp
from jax import lax
from jax.experimental import pallas as pl
from jax.experimental.pallas import tpu as pltpu
from jax.sharding import PartitionSpec as P

F32 = jnp.float32
BF16 = jnp.bfloat16
HEADDIM = 64
CHUNK = 128


def eye_flip(size):
    r = lax.broadcasted_iota(jnp.int32, (size, size), 0)
    c = lax.broadcasted_iota(jnp.int32, (size, size), 1)
    return jnp.where(r + c == size - 1, 1.0, 0.0).astype(BF16)


def flip_kernel(s_ref, o_ref):
    rows, width = s_ref.shape
    block = min(256, width)
    flip = eye_flip(block)
    count = width // block
    o_ref[:rows, :] = s_ref[...]
    for b in range(count):
        src = s_ref[:, (count - 1 - b) * block : (count - b) * block]
        o_ref[rows:, b * block : (b + 1) * block] = jnp.dot(
            src, flip, preferred_element_type=F32
        ).astype(BF16)


def stacked(sequence):
    rows, width = sequence.shape
    return pl.pallas_call(
        flip_kernel,
        out_shape=jax.ShapeDtypeStruct((2 * rows, width), BF16),
    )(sequence)


def pair_wide(cols, first):
    rows = cols.shape[0]
    lane = lax.broadcasted_iota(jnp.int32, (rows, 2 * HEADDIM), 1)
    return jnp.where(lane < HEADDIM, cols[:, first : first + 1], cols[:, first + 1 : first + 2])


def state_kernel(pairs, x_ref, b_ref, w_ref, o_ref):
    writer = b_ref[...]
    factor = w_ref[0]
    parts = []
    for p in range(pairs):
        x = x_ref[:, p * 128 : (p + 1) * 128].astype(F32)
        parts.append((x * pair_wide(factor, 2 * p)).astype(BF16))
    weighted = jnp.concatenate(parts, axis=1)
    o_ref[0] = lax.dot_general(
        writer, weighted, (((0,), (0,)), ((), ())), preferred_element_type=F32
    )


def local_states(inputs, state_proj, factor, rows):
    width = inputs.shape[1]
    state = state_proj.shape[1] // 2
    pairs = min(4, width // 128)
    groups = width // (128 * pairs)
    return pl.pallas_call(
        functools.partial(state_kernel, pairs),
        grid=(2, groups),
        in_specs=[
            pl.BlockSpec((rows, 128 * pairs), lambda d, g: (d, g)),
            pl.BlockSpec((rows, state), lambda d, g: (d, 0)),
            pl.BlockSpec((1, rows, 2 * pairs), lambda d, g: (d * groups + g, 0, 0)),
        ],
        out_specs=pl.BlockSpec((1, state, 128 * pairs), lambda d, g: (d, 0, g)),
        out_shape=jax.ShapeDtypeStruct((2, state, width), F32),
        compiler_params=pltpu.CompilerParams(dimension_semantics=("arbitrary", "arbitrary")),
    )(inputs, state_proj, factor)


def inside_kernel(pairs, state, x_ref, s_ref, ld_ref, ldt_ref, dt_ref, dtt_ref, skip_ref, o_ref, aff):
    branch = pl.program_id(0)
    rows = x_ref.shape[0]
    count = rows // CHUNK
    r = lax.broadcasted_iota(jnp.int32, (CHUNK, CHUNK), 0)
    c = lax.broadcasted_iota(jnp.int32, (CHUNK, CHUNK), 1)

    @pl.when(pl.program_id(1) == 0)
    def _():
        for k in range(count):
            at = slice(k * CHUNK, (k + 1) * CHUNK)
            aff[k] = lax.dot_general(
                s_ref[at, state:], s_ref[at, :state], (((1,), (1,)), ((), ())),
                preferred_element_type=F32,
            )

    lane = lax.broadcasted_iota(jnp.int32, (CHUNK, 128), 1)

    def run(ahead):
        keep = (r >= c) if ahead else (r <= c)
        ld = ld_ref[0]
        ldt = ldt_ref[0]
        dt = dt_ref[0]
        dtt = dtt_ref[0]
        order = range(count) if ahead else range(count - 1, -1, -1)
        carry = jnp.zeros((state, 128 * pairs), F32)
        edge_prev = None
        for step, k in enumerate(order):
            at = slice(k * CHUNK, (k + 1) * CHUNK)
            edge_row = (k + 1) * CHUNK - 1 if ahead else k * CHUNK
            ldk = ld[at, :]
            edge = ld[edge_row : edge_row + 1, :]
            since = jnp.exp(ldk) if step == 0 else jnp.exp(ldk - edge_prev)
            to_end = jnp.exp(edge - ldk) * dt[at, :]
            if step:
                carried = jnp.dot(s_ref[at, state:], carry.astype(BF16), preferred_element_type=F32)
            weighted = []
            for p in range(pairs):
                cols = slice(p * 128, (p + 1) * 128)
                x = x_ref[at, cols]
                xf = x.astype(F32)
                mixes = []
                for h in (2 * p, 2 * p + 1):
                    spread = jnp.where(keep, ldk[:, h : h + 1] - ldt[h : h + 1, at], 0.0)
                    mix = jnp.where(keep, aff[k] * jnp.exp(spread), 0.0) * dtt[h : h + 1, at]
                    mixes.append(mix.astype(BF16))
                zero = jnp.zeros_like(x)
                both = jnp.concatenate(
                    [jnp.where(lane < HEADDIM, x, zero), jnp.where(lane < HEADDIM, zero, x)], axis=0
                )
                out = jnp.dot(jnp.concatenate(mixes, axis=1), both, preferred_element_type=F32)
                out = out + xf * skip_ref[:, cols]
                if step:
                    out = out + carried[:, cols] * pair_wide(since, 2 * p)
                o_ref[at, cols] = out.astype(BF16)
                if step < count - 1:
                    weighted.append((xf * pair_wide(to_end, 2 * p)).astype(BF16))
            if step < count - 1:
                local = lax.dot_general(
                    s_ref[at, :state], jnp.concatenate(weighted, axis=1),
                    (((0,), (0,)), ((), ())), preferred_element_type=F32,
                )
                if step:
                    fade = jnp.exp(edge - edge_prev)
                    wide = jnp.concatenate([pair_wide(fade, 2 * p) for p in range(pairs)], axis=1)
                    carry = carry * wide + local
                else:
                    carry = local
            edge_prev = edge

    @pl.when(branch == 0)
    def _():
        run(True)

    @pl.when(branch == 1)
    def _():
        run(False)


def inside_of(inputs, state_proj, ld, ldt, dt, dtt, skip, rows):
    width = inputs.shape[1]
    state = state_proj.shape[1] // 2
    pairs = min(4, width // 128)
    groups = width // (128 * pairs)
    heads = 2 * pairs
    return pl.pallas_call(
        functools.partial(inside_kernel, pairs, state),
        grid=(2, groups),
        in_specs=[
            pl.BlockSpec((rows, 128 * pairs), lambda d, g: (d, g)),
            pl.BlockSpec((rows, 2 * state), lambda d, g: (d, 0)),
            pl.BlockSpec((1, rows, heads), lambda d, g: (d * groups + g, 0, 0)),
            pl.BlockSpec((1, heads, rows), lambda d, g: (d * groups + g, 0, 0)),
            pl.BlockSpec((1, rows, heads), lambda d, g: (d * groups + g, 0, 0)),
            pl.BlockSpec((1, heads, rows), lambda d, g: (d * groups + g, 0, 0)),
            pl.BlockSpec((1, 128 * pairs), lambda d, g: (0, g)),
        ],
        out_specs=pl.BlockSpec((rows, 128 * pairs), lambda d, g: (d, g)),
        out_shape=jax.ShapeDtypeStruct(inputs.shape, BF16),
        scratch_shapes=[pltpu.VMEM((rows // CHUNK, CHUNK, CHUNK), F32)],
        compiler_params=pltpu.CompilerParams(dimension_semantics=("arbitrary", "arbitrary")),
    )(inputs, state_proj, ld, ldt, dt, dtt, skip)


def gate_kernel(pairs, state, i_ref, g_ref, s_ref, ld_ref, c_ref, o_ref):
    reader = s_ref[:, state:]
    carried = jnp.dot(reader, c_ref[0].astype(BF16), preferred_element_type=F32)
    grown = jnp.exp(ld_ref[0])
    for p in range(pairs):
        cols = slice(p * 128, (p + 1) * 128)
        g = g_ref[:, cols].astype(F32)
        full = i_ref[:, cols].astype(F32) + carried[:, cols] * pair_wide(grown, 2 * p)
        o_ref[:, cols] = (full * (g / (1.0 + jnp.exp(-g)))).astype(BF16)


def gated_of(inside, gates, state_proj, ld, carry, rows):
    width = inside.shape[1]
    state = state_proj.shape[1] // 2
    pairs = min(4, width // 128)
    groups = width // (128 * pairs)
    heads = 2 * pairs
    tile = pl.BlockSpec((rows, 128 * pairs), lambda d, g: (d, g))
    return pl.pallas_call(
        functools.partial(gate_kernel, pairs, state),
        grid=(2, groups),
        in_specs=[
            tile,
            tile,
            pl.BlockSpec((rows, 2 * state), lambda d, g: (d, 0)),
            pl.BlockSpec((1, rows, heads), lambda d, g: (d * groups + g, 0, 0)),
            pl.BlockSpec((1, state, 128 * pairs), lambda d, g: (d, 0, g)),
        ],
        out_specs=tile,
        out_shape=jax.ShapeDtypeStruct(inside.shape, BF16),
        compiler_params=pltpu.CompilerParams(dimension_semantics=("arbitrary", "arbitrary")),
    )(inside, gates, state_proj, ld, carry)


def out_kernel(rows, at_ref, g_ref, w_ref, v_ref, o_ref):
    flipped = jnp.dot(v_ref[...], eye_flip(v_ref.shape[1]), preferred_element_type=F32).astype(BF16)
    acc = jnp.dot(g_ref[:rows, :], w_ref[...], preferred_element_type=F32)
    o_ref[...] = acc + jnp.dot(g_ref[rows:, :], flipped, preferred_element_type=F32)


def out_share(gated, weight, share, shares, rows):
    depth, columns = weight.shape
    wide = columns // shares
    block = min(256, wide)
    per = wide // block
    total = columns // block
    return pl.pallas_call(
        functools.partial(out_kernel, rows),
        grid_spec=pltpu.PrefetchScalarGridSpec(
            num_scalar_prefetch=1,
            grid=(per,),
            in_specs=[
                pl.BlockSpec(gated.shape, lambda j, at: (0, 0)),
                pl.BlockSpec((depth, block), lambda j, at: (0, at[0] * per + j)),
                pl.BlockSpec((depth, block), lambda j, at: (0, total - 1 - at[0] * per - j)),
            ],
            out_specs=pl.BlockSpec((rows, block), lambda j, at: (0, j)),
        ),
        out_shape=jax.ShapeDtypeStruct((rows, wide), F32),
        compiler_params=pltpu.CompilerParams(dimension_semantics=("arbitrary",)),
    )(share.reshape(1).astype(jnp.int32), gated, weight, weight)


def widen(logs):
    return jnp.repeat(jnp.exp(logs), HEADDIM, axis=-1)[..., None, :]


def entering(state, logs, axis):
    n = lax.axis_size(axis)
    me = lax.axis_index(axis)
    top = min(n, 4)
    strides = []
    d = 1
    while n // d > top:
        strides.append(d)
        d *= 2

    def span(first, length):
        return jnp.sum(lax.dynamic_slice_in_dim(logs, first, length, 0), axis=0)

    saved = []
    for d in strides:
        half = state.shape[1] // 2
        upper = (me // d) % 2
        low, high = state[:, :half], state[:, half:]
        mine = jnp.where(upper == 0, low, high)
        other = jnp.where(upper == 0, high, low)
        got = lax.ppermute(other, axis, [(i, i ^ d) for i in range(n)])
        x = jnp.where(upper == 0, mine, got)
        y = jnp.where(upper == 0, got, mine)
        base = (me // (2 * d)) * (2 * d)
        ax = widen(span(base, d))
        ay = widen(span(base + d, d))
        saved.append((d, upper, x, y, ax, ay))
        state = jnp.stack([ay[0] * x[0] + y[0], ax[1] * y[1] + x[1]])
    unit = n // top
    group = me // unit
    padded = jnp.concatenate([jnp.zeros((unit,) + logs.shape[1:], F32), logs,
                              jnp.zeros((unit,) + logs.shape[1:], F32)], axis=0)

    def padded_span(g):
        return jnp.sum(lax.dynamic_slice_in_dim(padded, (g + 1) * unit, unit, 0), axis=0)

    def shift(value, by):
        pairs = [(i, i + by * unit) for i in range(n) if 0 <= i + by * unit < n]
        return lax.ppermute(value, axis, pairs)

    own = padded_span(group)
    before = jnp.stack([padded_span(group - 1)[0], padded_span(group + 1)[1]])
    own_w = widen(own)
    entry = [shift(state[0], 1), shift(state[1], -1)]
    if top > 2:
        summed = [own_w[k] * entry[k] + state[k] for k in (0, 1)]
        fade = widen(before)
        far = [shift(summed[0], 2), shift(summed[1], -2)]
        entry = [fade[k] * far[k] + entry[k] for k in (0, 1)]
    enter = jnp.stack(entry)
    for d, upper, x, y, ax, ay in reversed(saved):
        low = jnp.stack([enter[0], ay[1] * enter[1] + y[1]])
        high = jnp.stack([ax[0] * enter[0] + x[0], enter[1]])
        mine = jnp.where(upper == 0, low, high)
        other = jnp.where(upper == 0, high, low)
        got = lax.ppermute(other, axis, [(i, i ^ d) for i in range(n)])
        enter = jnp.where(
            upper == 0,
            jnp.concatenate([mine, got], axis=1),
            jnp.concatenate([got, mine], axis=1),
        )
    return enter


def by_group(array, heads):
    two, rows, total = array.shape
    cols = array.reshape(two, rows, total // heads, heads)
    return (
        cols.transpose(0, 2, 1, 3).reshape(-1, rows, heads),
        cols.transpose(0, 2, 3, 1).reshape(-1, heads, rows),
    )


def on_device(
    sequence,
    input_weight,
    gate_weight,
    state_weight,
    step_weight,
    step_bias,
    decay_rate,
    skip_gain,
    output_weight,
):
    rows = sequence.shape[0]
    width = input_weight.shape[1]
    head_count = decay_rate.shape[0]
    group = 2 * min(4, width // 128)
    both = stacked(sequence)
    raw = jnp.dot(both, step_weight, preferred_element_type=F32) + step_bias[None, :]
    steps = jax.nn.softplus(raw).astype(BF16).astype(F32).reshape(2, rows, head_count)
    state_proj = jnp.dot(both, state_weight, preferred_element_type=F32).astype(BF16)
    r = lax.broadcasted_iota(jnp.int32, (rows, rows), 0)
    c = lax.broadcasted_iota(jnp.int32, (rows, rows), 1)
    tri = jnp.stack([(r >= c), (r <= c)]).astype(F32)
    ld = jnp.einsum(
        "bts,bsh->bth", tri, -decay_rate[None, None, :] * steps, precision=lax.Precision.HIGHEST
    )
    ends = jnp.stack([ld[0, -1], ld[1, 0]])
    logs = lax.all_gather(ends, "seq")
    factor = jnp.exp(ends[:, None, :] - ld) * steps
    ld_g, ldt_g = by_group(ld, group)
    dt_g, dtt_g = by_group(steps, group)
    factor_g, _ = by_group(factor, group)

    inputs = jnp.dot(both, input_weight, preferred_element_type=F32).astype(BF16)
    state = local_states(inputs, state_proj, factor_g, rows)
    carry = entering(state, logs, "seq")
    gates = jnp.dot(both, gate_weight, preferred_element_type=F32).astype(BF16)
    skip = jnp.repeat(skip_gain, HEADDIM)[None, :]
    inside = inside_of(inputs, state_proj, ld_g, ldt_g, dt_g, dtt_g, skip, rows)
    gated = gated_of(inside, gates, state_proj, ld_g, carry, rows)

    n = lax.axis_size("head")
    me = lax.axis_index("head")
    arrived = []
    for s in range(1, n):
        part = out_share(gated, output_weight, lax.rem(me + s, n), n, rows)
        arrived.append(lax.ppermute(part, "head", [(i, (i + s) % n) for i in range(n)]))
    total = out_share(gated, output_weight, me, n, rows)
    for part in arrived:
        total = total + part
    return total.astype(BF16)


def solution(mesh):
    placed = (
        P("seq", None),
        P(None, "head"),
        P(None, "head"),
        P(),
        P(None, "head"),
        P("head"),
        P("head"),
        P("head"),
        P("head", None),
    )
    return jax.shard_map(
        on_device, mesh=mesh, in_specs=placed, out_specs=P("seq", "head"), check_vma=False
    )
```

profile of v0, /device:TPU:0, one launch (start us, length us, event | category | flops | bytes accessed | tf_op | source)
XLA Modules:
  0.0 218.9 jit_solution(9822595803559328368)
XLA Ops:
  0.0 0.2 iota_compare_fusion
  0.2 4.4 %shard_map.91 = bf16[1024,2048]{1,0:T(8,128)(2,1)} custom-call(bf16[512,2048]{1,0:T(8,128)(2,1)} %s_ref.1), custom_call_target="tpu_custom_call" | custom-call | tf_op jit(solution)/shard_map/pallas_call | solution.py:37
  4.6 14.8 %convolution_convert_fusion.1.x_ref = bf16[1024,2048]{1,0:T(8,128)(2,1)} fusion(bf16[1024,2048]{1,0:T(8,128)(2,1)} %shard_map.91, bf16[2048,2048]{1,0:T(8,128)(2,1)} %param.10), kind=kOutput, calls=%fused_computation.1 | convolution fusion | flops 8592031744 | bytes 16777216 | tf_op jit(solution)/shard_map/dot_general | solution.py:357
  19.4 2.1 convolution_convert_fusion.2.s_ref.b_ref
  21.5 1.4 fusion.9
  22.9 1.0 fusion
  23.9 0.2 slice_reduce_fusion.1
  24.1 0.1 bitcast_multiply_fusion
  24.3 1.9 copy.27
  26.2 10.0 %shard_map.93 = f32[2,128,2048]{2,1,0:T(8,128)} custom-call(bf16[1024,2048]{1,0:T(8,128)(2,1)} %convolution_convert_fusion.1.x_ref, bf16[1024,256]{1,0:T(8,128)(2,1)} %convolution_convert_fusion.2.s_ref.b_ref, f32[8,512,8]{2,1,0:T(8,128)} %bitcast.87), custom_call_target="tpu_custom_call" | custom-call | tf_op jit(solution)/shard_map/pallas_call | solution.py:67
  36.2 1.8 slice_select_fusion
  38.0 0.6 collective-permute-start
  38.6 22.7 %all-gather.1 = f32[16,2,32]{2,1,0:T(2,128)S(1)} all-gather(f32[1,2,32]{2,1,0:T(2,128)S(1)} %get-tuple-element.54), channel_id=2, replica_groups=mesh['seq'=16,'head'=2] {'seq'}, dimensions={0}, use_global_device_ids=true | all-gather | bytes 4352 | tf_op jit(solution)/shard_map/all_gather | solution.py:351
  61.4 0.1 broadcast_in_dim.68
  61.5 0.1 broadcast_in_dim.69
  61.6 0.1 broadcast_in_dim.70
  61.7 0.1 broadcast_in_dim.66
  61.8 1.4 broadcast_select_fusion
  63.3 1.0 copy-done.5
  64.2 0.2 slice_add_fusion.1
  64.8 14.0 %collective-permute-done.1 = f32[2,32,2048]{2,1,0:T(8,128)} collective-permute-done((f32[2,32,2048]{2,1,0:T(8,128)S(1)}, f32[2,32,2048]{2,1,0:T(8,128)}, u32[]{:S(2)}, u32[]{:S(2)}) %collective-permute-start.1) | collective-permute-done | bytes 524320 | tf_op jit(solution)/shard_map/ppermute | solution.py:272
  78.8 1.1 broadcast_select_fusion.2
  80.0 1.3 collective-permute-start.4
  82.2 4.6 %collective-permute-start.2 = (f32[32,2048]{1,0:T(8,128)S(1)}, f32[32,2048]{1,0:T(8,128)S(1)}, u32[]{:S(2)}, u32[]{:S(2)}) collective-permute-start(f32[32,2048]{1,0:T(8,128)S(1)} %get-tuple-element.26), channel_id=1, source_target_pairs={{0,8},{2,10},{4,12},{6,14},{8,16},{10,18},{12,20},{14,22},{16,24},... | collective-permute-start | bytes 786440 | tf_op jit(solution)/shard_map/ppermute | solution.py:290
  86.8 2.8 %collective-permute-done.4 = f32[32,2048]{1,0:T(8,128)S(1)} collective-permute-done((f32[32,2048]{1,0:T(8,128)S(1)}, f32[32,2048]{1,0:T(8,128)S(1)}, u32[]{:S(2)}, u32[]{:S(2)}) %collective-permute-start.4) | collective-permute-done | bytes 262176 | tf_op jit(solution)/shard_map/ppermute | solution.py:290
  89.7 1.3 collective-permute-start.5
  91.0 0.7 collective-permute-done.2
  91.7 4.7 %collective-permute-start.3 = (f32[32,2048]{1,0:T(8,128)S(1)}, f32[32,2048]{1,0:T(8,128)S(1)}, u32[]{:S(2)}, u32[]{:S(2)}) collective-permute-start(f32[32,2048]{1,0:T(8,128)S(1)} %multiply_add_fusion.5), channel_id=1, source_target_pairs={{0,16},{2,18},{4,20},{6,22},{8,24},{10,26},{12,28},{14,30},{1,17},... | collective-permute-start | bytes 786440 | tf_op jit(solution)/shard_map/ppermute | solution.py:290
  96.5 7.4 %collective-permute-done.5 = f32[32,2048]{1,0:T(8,128)S(1)} collective-permute-done((f32[32,2048]{1,0:T(8,128)S(1)}, f32[32,2048]{1,0:T(8,128)S(1)}, u32[]{:S(2)}, u32[]{:S(2)}) %collective-permute-start.5) | collective-permute-done | bytes 262176 | tf_op jit(solution)/shard_map/ppermute | solution.py:290
  104.0 0.9 fusion.5
  104.9 0.8 collective-permute-start.6
  105.8 1.9 copy.24
  107.7 0.6 copy.25
  108.4 1.9 copy.23
  110.4 0.7 broadcast_in_dim_reshape.2.skip_ref
  111.4 17.8 %shard_map.92.i_ref = bf16[1024,2048]{1,0:T(8,128)(2,1)} custom-call(bf16[1024,2048]{1,0:T(8,128)(2,1)} %convolution_convert_fusion.1.x_ref, bf16[1024,256]{1,0:T(8,128)(2,1)} %convolution_convert_fusion.2.s_ref.b_ref, f32[8,512,8]{2,1,0:T(8,128)} %bitcast.85, f32[8,8,512]{2,1,0:T(8,128)} %bitcast.93, f32[8,512,8]{2,1,0:T(8,128)} %bitcast.88, ...), custom_call_target="tpu_custom_call" | custom-call | tf_op jit(solution)/shard_map/pallas_call | solution.py:166
  129.2 0.1 maximum_select_fusion.1
  129.3 0.2 fusion.18
  129.5 0.1 fusion.2
  129.7 1.7 copy-done.3
  131.4 12.6 %convolution_convert_fusion.g_ref = bf16[1024,2048]{1,0:T(8,128)(2,1)} fusion(bf16[1024,2048]{1,0:T(8,128)(2,1)S(1)} %copy-done.3, bf16[2048,2048]{1,0:T(8,128)(2,1)} %param.11), kind=kOutput, calls=%fused_computation | convolution fusion | flops 8592031744 | bytes 16777216 | tf_op jit(solution)/shard_map/dot_general | solution.py:360
  144.0 1.5 maximum_select_fusion.c_ref
  145.6 10.8 %shard_map.94.g_ref = bf16[1024,2048]{1,0:T(8,128)(2,1)} custom-call(bf16[1024,2048]{1,0:T(8,128)(2,1)} %shard_map.92.i_ref, bf16[1024,2048]{1,0:T(8,128)(2,1)} %convolution_convert_fusion.g_ref, bf16[1024,256]{1,0:T(8,128)(2,1)} %convolution_convert_fusion.2.s_ref.b_ref, f32[8,512,8]{2,1,0:T(8,128)} %bitcast.86, f32[2,128,2048]{2,1,0:T(8,128)} %maximum_select_fusion.c_ref), custom_call_target="tpu_custom_call" | custom-call | tf_op jit(solution)/shard_map/pallas_call | solution.py:203
  156.4 12.2 %shard_map.96 = f32[512,1024]{1,0:T(8,128)} custom-call(s32[1]{0:T(128)} %bitcast.32.at_ref, bf16[1024,2048]{1,0:T(8,128)(2,1)} %shard_map.94.g_ref, bf16[2048,2048]{1,0:T(8,128)(2,1)} %v_ref.3, bf16[2048,2048]{1,0:T(8,128)(2,1)} %v_ref.3), custom_call_target="tpu_custom_call" | custom-call | tf_op jit(solution)/shard_map/pallas_call | solution.py:231
  168.6 1.5 collective-permute-start.8
  170.1 12.3 %shard_map.95 = f32[512,1024]{1,0:T(8,128)} custom-call(s32[1]{0:T(128)} %bitcast.at_ref, bf16[1024,2048]{1,0:T(8,128)(2,1)} %shard_map.94.g_ref, bf16[2048,2048]{1,0:T(8,128)(2,1)} %v_ref.3, bf16[2048,2048]{1,0:T(8,128)(2,1)} %v_ref.3), custom_call_target="tpu_custom_call" | custom-call | tf_op jit(solution)/shard_map/pallas_call | solution.py:231
  182.4 33.7 %collective-permute-done.8 = f32[512,1024]{1,0:T(8,128)S(1)} collective-permute-done((f32[512,1024]{1,0:T(8,128)}, f32[512,1024]{1,0:T(8,128)S(1)}, u32[]{:S(2)}, u32[]{:S(2)}) %collective-permute-start.8) | collective-permute-done | bytes 2097184 | tf_op jit(solution)/shard_map/ppermute | solution.py:370
  216.1 2.9 %add_convert_fusion = bf16[512,1024]{1,0:T(8,128)(2,1)} fusion(f32[512,1024]{1,0:T(8,128)} %shard_map.95, f32[512,1024]{1,0:T(8,128)S(1)} %collective-permute-done.8), kind=kLoop, calls=%fused_computation.3 | loop fusion | flops 1048576 | bytes 5242880 | tf_op jit(solution)/shard_map/convert_element_type | solution.py:374
  (78 shorter events, 2.2 us)
Async XLA Ops:
  0.0 19.4 %copy-start = (bf16[2048,256]{1,0:T(8,128)(2,1)S(1)}, bf16[2048,256]{1,0:T(8,128)(2,1)}, u32[]{:S(2)}) copy-start(bf16[2048,256]{1,0:T(8,128)(2,1)} %param.12) | copy-start | bytes 3145732
  4.6 14.8 %copy-start.2 = (bf16[1024,2048]{1,0:T(8,128)(2,1)S(1)}, bf16[1024,2048]{1,0:T(8,128)(2,1)}, u32[]{:S(2)}) copy-start(bf16[1024,2048]{1,0:T(8,128)(2,1)} %shard_map.91) | copy-start | bytes 12582916
  19.4 2.1 copy-start.11
  19.4 2.1 copy-start.8
  19.4 2.1 copy-start.9
  23.9 84.4 %copy-start.7 = (f32[2,512,32]{1,2,0:T(8,128)}, f32[2,512,32]{1,2,0:T(8,128)S(1)}, u32[]{:S(2)}) copy-start(f32[2,512,32]{1,2,0:T(8,128)S(1)} %fusion) | copy-start | bytes 393220
  36.2 25.6 %copy-start.4 = (f32[2,128,2048]{2,1,0:T(8,128)S(1)}, f32[2,128,2048]{2,1,0:T(8,128)}, u32[]{:S(2)}) copy-start(f32[2,128,2048]{2,1,0:T(8,128)} %shard_map.93) | copy-start | bytes 6291460
  38.0 23.8 %collective-permute-start = (f32[2,64,2048]{2,1,0:T(8,128)S(1)}, f32[2,64,2048]{2,1,0:T(8,128)}, u32[]{:S(2)}, u32[]{:S(2)}) collective-permute-start(f32[2,64,2048]{2,1,0:T(8,128)S(1)} %slice_select_fusion), channel_id=1, source_target_pairs={{0,2},{2,0},{4,6},{6,4},{8,10},{10,8},{12,14},{14,12},{16,18},{18,... | collective-permute-start | bytes 3145736 | tf_op jit(solution)/shard_map/ppermute | solution.py:272
  63.3 1.0 copy-start.5
  64.5 14.3 %collective-permute-start.1 = (f32[2,32,2048]{2,1,0:T(8,128)S(1)}, f32[2,32,2048]{2,1,0:T(8,128)}, u32[]{:S(2)}, u32[]{:S(2)}) collective-permute-start(f32[2,32,2048]{2,1,0:T(8,128)S(1)} %broadcast_select_fusion.4), channel_id=1, source_target_pairs={{0,4},{2,6},{4,0},{6,2},{8,12},{10,14},{12,8},{14,10},{16,20},{18,... | collective-permute-start | bytes 1572872 | tf_op jit(solution)/shard_map/ppermute | solution.py:272
  80.0 9.6 %collective-permute-start.4 = (f32[32,2048]{1,0:T(8,128)S(1)}, f32[32,2048]{1,0:T(8,128)S(1)}, u32[]{:S(2)}, u32[]{:S(2)}) collective-permute-start(f32[32,2048]{1,0:T(8,128)S(1)} %get-tuple-element.27), channel_id=1, source_target_pairs={{8,0},{10,2},{12,4},{14,6},{16,8},{18,10},{20,12},{22,14},{24,16},... | collective-permute-start | bytes 786440 | tf_op jit(solution)/shard_map/ppermute | solution.py:290
  82.2 9.5 %collective-permute-start.2 = (f32[32,2048]{1,0:T(8,128)S(1)}, f32[32,2048]{1,0:T(8,128)S(1)}, u32[]{:S(2)}, u32[]{:S(2)}) collective-permute-start(f32[32,2048]{1,0:T(8,128)S(1)} %get-tuple-element.26), channel_id=1, source_target_pairs={{0,8},{2,10},{4,12},{6,14},{8,16},{10,18},{12,20},{14,22},{16,24},... | collective-permute-start | bytes 786440 | tf_op jit(solution)/shard_map/ppermute | solution.py:290
  89.7 14.2 %collective-permute-start.5 = (f32[32,2048]{1,0:T(8,128)S(1)}, f32[32,2048]{1,0:T(8,128)S(1)}, u32[]{:S(2)}, u32[]{:S(2)}) collective-permute-start(f32[32,2048]{1,0:T(8,128)S(1)} %multiply_add_fusion.3), channel_id=1, source_target_pairs={{16,0},{18,2},{20,4},{22,6},{24,8},{26,10},{28,12},{30,14},{17,1},... | collective-permute-start | bytes 786440 | tf_op jit(solution)/shard_map/ppermute | solution.py:290
  91.7 12.2 %collective-permute-start.3 = (f32[32,2048]{1,0:T(8,128)S(1)}, f32[32,2048]{1,0:T(8,128)S(1)}, u32[]{:S(2)}, u32[]{:S(2)}) collective-permute-start(f32[32,2048]{1,0:T(8,128)S(1)} %multiply_add_fusion.5), channel_id=1, source_target_pairs={{0,16},{2,18},{4,20},{6,22},{8,24},{10,26},{12,28},{14,30},{1,17},... | collective-permute-start | bytes 786440 | tf_op jit(solution)/shard_map/ppermute | solution.py:290
  104.0 6.4 %copy-start.10 = (f32[32]{0:T(128)S(1)}, f32[32]{0:T(128)}, u32[]{:S(2)}) copy-start(f32[32]{0:T(128)} %param.16) | copy-start | bytes 388
  104.9 24.2 %collective-permute-start.6 = (f32[2,32,2048]{2,1,0:T(8,128)}, f32[2,32,2048]{2,1,0:T(8,128)S(1)}, u32[]{:S(2)}, u32[]{:S(2)}) collective-permute-start(f32[2,32,2048]{2,1,0:T(8,128)} %get-tuple-element.25), channel_id=1, source_target_pairs={{0,4},{2,6},{4,0},{6,2},{8,12},{10,14},{12,8},{14,10},{16,20},{18,... | collective-permute-start | bytes 1572872 | tf_op jit(solution)/shard_map/ppermute | solution.py:307
  111.4 17.9 %copy-start.6 = (f32[2,64,2048]{2,1,0:T(8,128)S(1)}, f32[2,64,2048]{2,1,0:T(8,128)}, u32[]{:S(2)}) copy-start(f32[2,64,2048]{2,1,0:T(8,128)} %copy-done.5) | copy-start | bytes 3145732
  129.3 2.2 copy-start.3
  129.6 14.4 %collective-permute-start.7 = (f32[2,64,2048]{2,1,0:T(8,128)S(1)}, f32[2,64,2048]{2,1,0:T(8,128)S(1)}, u32[]{:S(2)}, u32[]{:S(2)}) collective-permute-start(f32[2,64,2048]{2,1,0:T(8,128)S(1)} %get-tuple-element.15), channel_id=1, source_target_pairs={{0,2},{2,0},{4,6},{6,4},{8,10},{10,8},{12,14},{14,12},{16,18},{18,... | collective-permute-start | bytes 3145736 | tf_op jit(solution)/shard_map/ppermute | solution.py:307
  168.6 47.5 %collective-permute-start.8 = (f32[512,1024]{1,0:T(8,128)}, f32[512,1024]{1,0:T(8,128)S(1)}, u32[]{:S(2)}, u32[]{:S(2)}) collective-permute-start(f32[512,1024]{1,0:T(8,128)} %shard_map.96), channel_id=1, source_target_pairs={{0,1},{1,0},{2,3},{3,2},{4,5},{5,4},{6,7},{7,6},{8,9},{9,8},{10,11... | collective-permute-start | bytes 6291464 | tf_op jit(solution)/shard_map/ppermute | solution.py:370
  170.1 48.8 %copy-start.1 = (bf16[2048,256]{1,0:T(8,128)(2,1)S(1)}, bf16[2048,256]{1,0:T(8,128)(2,1)}, u32[]{:S(2)}) copy-start(bf16[2048,256]{1,0:T(8,128)(2,1)} %param.12) | copy-start | bytes 3145732
where the time goes:
time: 220 us; the launch traced here: 219 us
  Pallas kernels  67.4 us (31%)
  waiting for transfers between devices  58.7 us (27%)
  matrix products  31.9 us (14%)
  blocking collectives  22.7 us (10%)
  starting transfers between devices  14.9 us (7%)
  local copies, waits for them, and re-layouts  11.9 us (5%)
  other arithmetic  11 us (5%)
    ppermute x1, waiting for transfers between devices, on_device(): lax.ppermute(part, 'head', [(i, (i + s) % n) for i in range(n)])  33.7 us
    pallas_call x2, Pallas kernels, out_share(): pl.pallas_call(functools.partial(out_kernel, rows), grid_spec=pltpu.Prefe...  24.5 us
    all_gather x1, blocking collectives, on_device(): logs = lax.all_gather(ends, 'seq')  22.7 us
    pallas_call x1, Pallas kernels, inside_of(): pl.pallas_call(functools.partial(inside_kernel, pairs, state), grid=(2, g...  17.8 us
    dot_general x1, matrix products, on_device(): jnp.dot(both, input_weight, preferred_element_type=F32).astype(BF16)  14.8 us
    ppermute x4, waiting for transfers between devices, entering(): got = lax.ppermute(other, axis, [(i, i ^ d) for i in range(n)])  14 us
    dot_general x1, matrix products, on_device(): gates = jnp.dot(both, gate_weight, preferred_element_type=F32).astype(BF16)  12.6 us
    ppermute x4, starting transfers between devices, shift(): return lax.ppermute(value, axis, pairs)  11.9 us
  transfers between devices with their start and end apart: 9, of which 5 were waited for; matrix products, arithmetic and copies ran while one was open for 9% of the time, Pallas kernels for 14%

commit v1 on v0

--- a/solution.py
+++ b/solution.py
@@ -249,7 +249,7 @@
     return jnp.repeat(jnp.exp(logs), HEADDIM, axis=-1)[..., None, :]
 
 
-def entering(state, logs, axis):
+def entering(state, own, gate_of, inside_from, axis):
     n = lax.axis_size(axis)
     me = lax.axis_index(axis)
     top = min(n, 4)
@@ -259,11 +259,11 @@
         strides.append(d)
         d *= 2
 
-    def span(first, length):
-        return jnp.sum(lax.dynamic_slice_in_dim(logs, first, length, 0), axis=0)
-
     saved = []
+    tied = None if strides else gate_of(state)[1]
     for d in strides:
+        if d == strides[-1]:
+            state, tied = gate_of(state)
         half = state.shape[1] // 2
         upper = (me // d) % 2
         low, high = state[:, :half], state[:, half:]
@@ -272,25 +272,21 @@
         got = lax.ppermute(other, axis, [(i, i ^ d) for i in range(n)])
         x = jnp.where(upper == 0, mine, got)
         y = jnp.where(upper == 0, got, mine)
-        base = (me // (2 * d)) * (2 * d)
-        ax = widen(span(base, d))
-        ay = widen(span(base + d, d))
+        got_log = lax.ppermute(own, axis, [(i, i ^ d) for i in range(n)])
+        ax = widen(jnp.where(upper == 0, own, got_log))
+        ay = widen(jnp.where(upper == 0, got_log, own))
+        own = own + got_log
         saved.append((d, upper, x, y, ax, ay))
         state = jnp.stack([ay[0] * x[0] + y[0], ax[1] * y[1] + x[1]])
     unit = n // top
-    group = me // unit
-    padded = jnp.concatenate([jnp.zeros((unit,) + logs.shape[1:], F32), logs,
-                              jnp.zeros((unit,) + logs.shape[1:], F32)], axis=0)
-
-    def padded_span(g):
-        return jnp.sum(lax.dynamic_slice_in_dim(padded, (g + 1) * unit, unit, 0), axis=0)
+    gates = tied
+    state, gates = lax.optimization_barrier((state, gates))
 
     def shift(value, by):
         pairs = [(i, i + by * unit) for i in range(n) if 0 <= i + by * unit < n]
         return lax.ppermute(value, axis, pairs)
 
-    own = padded_span(group)
-    before = jnp.stack([padded_span(group - 1)[0], padded_span(group + 1)[1]])
+    before = jnp.stack([shift(own[0], 1), shift(own[1], -1)])
     own_w = widen(own)
     entry = [shift(state[0], 1), shift(state[1], -1)]
     if top > 2:
@@ -299,18 +295,23 @@
         far = [shift(summed[0], 2), shift(summed[1], -2)]
         entry = [fade[k] * far[k] + entry[k] for k in (0, 1)]
     enter = jnp.stack(entry)
+    enter, inside = inside_from(enter)
+    first = True
     for d, upper, x, y, ax, ay in reversed(saved):
         low = jnp.stack([enter[0], ay[1] * enter[1] + y[1]])
         high = jnp.stack([ax[0] * enter[0] + x[0], enter[1]])
         mine = jnp.where(upper == 0, low, high)
         other = jnp.where(upper == 0, high, low)
+        if not first:
+            other, inside = lax.optimization_barrier((other, inside))
+        first = False
         got = lax.ppermute(other, axis, [(i, i ^ d) for i in range(n)])
         enter = jnp.where(
             upper == 0,
             jnp.concatenate([mine, got], axis=1),
             jnp.concatenate([got, mine], axis=1),
         )
-    return enter
+    return enter, gates, inside
 
 
 def by_group(array, heads):
@@ -348,7 +349,6 @@
         "bts,bsh->bth", tri, -decay_rate[None, None, :] * steps, precision=lax.Precision.HIGHEST
     )
     ends = jnp.stack([ld[0, -1], ld[1, 0]])
-    logs = lax.all_gather(ends, "seq")
     factor = jnp.exp(ends[:, None, :] - ld) * steps
     ld_g, ldt_g = by_group(ld, group)
     dt_g, dtt_g = by_group(steps, group)
@@ -356,18 +356,30 @@
 
     inputs = jnp.dot(both, input_weight, preferred_element_type=F32).astype(BF16)
     state = local_states(inputs, state_proj, factor_g, rows)
-    carry = entering(state, logs, "seq")
-    gates = jnp.dot(both, gate_weight, preferred_element_type=F32).astype(BF16)
     skip = jnp.repeat(skip_gain, HEADDIM)[None, :]
-    inside = inside_of(inputs, state_proj, ld_g, ldt_g, dt_g, dtt_g, skip, rows)
+
+    def gate_of(after):
+        after, source = lax.optimization_barrier((after, both))
+        return after, jnp.dot(source, gate_weight, preferred_element_type=F32).astype(BF16)
+
+    def inside_from(after):
+        after, source = lax.optimization_barrier((after, inputs))
+        return after, inside_of(source, state_proj, ld_g, ldt_g, dt_g, dtt_g, skip, rows)
+
+    carry, gates, inside = entering(state, ends, gate_of, inside_from, "seq")
     gated = gated_of(inside, gates, state_proj, ld_g, carry, rows)
 
     n = lax.axis_size("head")
     me = lax.axis_index("head")
     arrived = []
+    cuts = 2
     for s in range(1, n):
-        part = out_share(gated, output_weight, lax.rem(me + s, n), n, rows)
-        arrived.append(lax.ppermute(part, "head", [(i, (i + s) % n) for i in range(n)]))
+        peer = lax.rem(me + s, n)
+        pieces = []
+        for k in range(cuts):
+            part = out_share(gated, output_weight, cuts * peer + k, cuts * n, rows)
+            pieces.append(lax.ppermute(part, "head", [(i, (i + s) % n) for i in range(n)]))
+        arrived.append(jnp.concatenate(pieces, axis=1))
     total = out_share(gated, output_weight, me, n, rows)
     for part in arrived:
         total = total + part

time: 220 us -> 193 us (0.88)
  blocking collectives: 22.7 us -> 0 us
  waiting for transfers between devices: 58.7 us -> 36.6 us
  starting transfers between devices: 14.9 us -> 28 us
  Pallas kernels: 67.4 us -> 71.2 us
  matrix products: 31.9 us -> 34.3 us
    all_gather x1 -> x0, blocking collectives: 22.7 us -> none  [on_device(): logs = lax.all_gather(ends, 'seq')]
    ppermute x4, waiting for transfers between devices: 14 us -> 2.65 us  [entering(): got = lax.ppermute(other, axis, [(i, i ^ d) for i in range(n)])]
    ppermute x1 -> x2, waiting for transfers between devices: 33.7 us -> 25.7 us  [on_device(): lax.ppermute(part, 'head', [(i, (i + s) % n) for i in range(n)])]
    ppermute x4 -> x6, starting transfers between devices: 11.9 us -> 18.4 us  [shift(): return lax.ppermute(value, axis, pairs)]
    ppermute x4 -> x6, waiting for transfers between devices: 11 us -> 7.05 us  [shift(): return lax.ppermute(value, axis, pairs)]
    pallas_call x2 -> x3, Pallas kernels: 24.5 us -> 28.1 us  [out_share(): pl.pallas_call(functools.partial(out_kernel, rows), grid_spec=pltpu.Prefe...]
    ppermute x0 -> x2, starting transfers between devices: none -> 3.59 us  [entering(): got_log = lax.ppermute(own, axis, [(i, i ^ d) for i in range(n)])]
    select_n x2 -> x1, other arithmetic: 2.58 us -> 0.09 us  [entering(): y = jnp.where(upper == 0, got, mine)]
  transfers between devices with their start and end apart: 9 -> 14, of which waited for: 5 -> 5; matrix products, arithmetic and copies ran while one was open for 9% -> 21% of each run, Pallas kernels for 14% -> 25%
where the time goes in v1:
time: 193 us; the launch traced here: 192 us
  Pallas kernels  71.2 us (37%)
  waiting for transfers between devices  36.6 us (19%)
  matrix products  34.3 us (18%)
  starting transfers between devices  28 us (15%)
  other arithmetic  10.6 us (5%)
  local copies, waits for them, and re-layouts  10.4 us (5%)
    pallas_call x3, Pallas kernels, out_share(): pl.pallas_call(functools.partial(out_kernel, rows), grid_spec=pltpu.Prefe...  28.1 us
    ppermute x2, waiting for transfers between devices, on_device(): lax.ppermute(part, 'head', [(i, (i + s) % n) for i in range(n)])  25.7 us
    ppermute x6, starting transfers between devices, shift(): return lax.ppermute(value, axis, pairs)  18.4 us
    pallas_call x1, Pallas kernels, inside_of(): pl.pallas_call(functools.partial(inside_kernel, pairs, state), grid=(2, g...  18 us
    dot_general x1, matrix products, on_device(): jnp.dot(both, input_weight, preferred_element_type=F32).astype(BF16)  15 us
    dot_general x1, matrix products, gate_of(): jnp.dot(source, gate_weight, preferred_element_type=F32).astype(BF16)  12.6 us
    pallas_call x1, Pallas kernels, gated_of(): pl.pallas_call(functools.partial(gate_kernel, pairs, state), grid=(2, gro...  10.8 us
    pallas_call x1, Pallas kernels, local_states(): pl.pallas_call(functools.partial(state_kernel, pairs), grid=(2, groups),...  9.96 us
  transfers between devices with their start and end apart: 14, of which 5 were waited for; matrix products, arithmetic and copies ran while one was open for 21% of the time, Pallas kernels for 25%

profile of v1, /device:TPU:0, one launch (start us, length us, event | category | flops | bytes accessed | tf_op | source)
XLA Modules:
  0.0 191.7 jit_solution(2157700845184284323)
XLA Ops:
  0.0 0.2 iota_compare_fusion
  0.2 4.3 %shard_map.91 = bf16[1024,2048]{1,0:T(8,128)(2,1)} custom-call(bf16[512,2048]{1,0:T(8,128)(2,1)} %s_ref.1), custom_call_target="tpu_custom_call" | custom-call | tf_op jit(solution)/shard_map/pallas_call | solution.py:37
  4.6 3.6 %fusion.7 = f32[1024,32]{0,1:T(8,128)S(1)} fusion(bf16[1024,2048]{1,0:T(8,128)(2,1)} %shard_map.91, bf16[2048,32]{0,1:T(8,128)(2,1)S(1)} %copy-done.10, f32[32]{0:T(128)S(1)} %copy-done.11), kind=kOutput, calls=%fused_computation.51 | convolution fusion | flops 134512640 | bytes 4456576 | tf_op jit(solution)/shard_map/dot_general | solution.py:342
  8.1 1.0 fusion.1
  9.2 0.2 slice_reduce_fusion.1
  9.4 0.6 collective-permute-start
  10.1 15.0 %convolution_convert_fusion.1.x_ref = bf16[1024,2048]{1,0:T(8,128)(2,1)} fusion(bf16[1024,2048]{1,0:T(8,128)(2,1)} %shard_map.91, bf16[2048,2048]{1,0:T(8,128)(2,1)} %param.10), kind=kOutput, calls=%fused_computation.1 | convolution fusion | flops 8592031744 | bytes 16777216 | tf_op jit(solution)/shard_map/dot_general | solution.py:357
  25.1 2.1 %convolution_convert_fusion.2.b_ref.s_ref = bf16[1024,256]{1,0:T(8,128)(2,1)} fusion(bf16[1024,2048]{1,0:T(8,128)(2,1)S(1)} %copy-done.2, bf16[2048,256]{1,0:T(8,128)(2,1)S(1)} %copy-done), kind=kOutput, calls=%fused_computation.7 | convolution fusion | flops 1074003968 | bytes 5767168 | tf_op jit(solution)/shard_map/dot_general | solution.py:344
  27.2 2.0 %copy.18 = f32[2,2048,8]{2,1,0:T(8,128)} copy(f32[2,2048,8]{1,2,0:T(8,128)S(1)} %pad_maximum_fusion.7) | data formatting | bytes 262144 | tf_op jit(solution)/shard_map/concatenate
  29.2 10.0 %shard_map.92 = f32[2,128,2048]{2,1,0:T(8,128)} custom-call(bf16[1024,2048]{1,0:T(8,128)(2,1)} %convolution_convert_fusion.1.x_ref, bf16[1024,256]{1,0:T(8,128)(2,1)} %convolution_convert_fusion.2.b_ref.s_ref, f32[8,512,8]{2,1,0:T(8,128)} %bitcast.76), custom_call_target="tpu_custom_call" | custom-call | tf_op jit(solution)/shard_map/pallas_call | solution.py:67
  39.2 1.8 slice_select_fusion
  41.1 3.0 %collective-permute-start.1 = (f32[2,32]{1,0:T(2,128)S(1)}, f32[2,32]{1,0:T(2,128)S(1)}, u32[]{:S(2)}, u32[]{:S(2)}) collective-permute-start(f32[2,32]{1,0:T(2,128)S(1)} %get-tuple-element.59), channel_id=1, source_target_pairs={{0,4},{2,6},{4,0},{6,2},{8,12},{10,14},{12,8},{14,10},{16,20},{18,... | collective-permute-start | bytes 776 | tf_op jit(solution)/shard_map/ppermute | solution.py:275
  44.4 1.3 collective-permute-done.1
  46.0 1.4 broadcast_select_fusion.1
  47.5 0.2 slice_add_fusion.1
  47.7 0.8 copy-done.5
  48.4 0.4 copy-done.7
  48.9 2.1 %collective-permute-start.5 = (f32[2,32,2048]{2,1,0:T(8,128)S(1)}, f32[2,32,2048]{2,1,0:T(8,128)S(1)}, u32[]{:S(2)}, u32[]{:S(2)}) collective-permute-start(f32[2,32,2048]{2,1,0:T(8,128)S(1)} %slice_select_fusion.2), channel_id=1, source_target_pairs={{0,4},{2,6},{4,0},{6,2},{8,12},{10,14},{12,8},{14,10},{16,20},{18,... | collective-permute-start | bytes 1572872 | tf_op jit(solution)/shard_map/ppermute | solution.py:272
  51.0 12.6 %convolution_convert_fusion.g_ref = bf16[1024,2048]{1,0:T(8,128)(2,1)} fusion(bf16[1024,2048]{1,0:T(8,128)(2,1)S(1)} %copy-done.3, bf16[2048,2048]{1,0:T(8,128)(2,1)} %param.11), kind=kOutput, calls=%fused_computation | convolution fusion | flops 8592031744 | bytes 16777216 | tf_op jit(solution)/shard_map/dot_general | solution.py:363
  63.9 1.3 collective-permute-start.8
  65.2 4.6 %collective-permute-start.6 = (f32[32,2048]{1,0:T(8,128)S(1)}, f32[32,2048]{1,0:T(8,128)S(1)}, u32[]{:S(2)}, u32[]{:S(2)}) collective-permute-start(f32[32,2048]{1,0:T(8,128)S(1)} %get-tuple-element.47), channel_id=1, source_target_pairs={{0,8},{2,10},{4,12},{6,14},{8,16},{10,18},{12,20},{14,22},{16,24},... | collective-permute-start | bytes 786440 | tf_op jit(solution)/shard_map/ppermute | solution.py:287
  70.1 1.3 collective-permute-start.3
  71.4 4.5 %collective-permute-start.2 = (f32[32]{0:T(128)S(1)}, f32[32]{0:T(128)S(1)}, u32[]{:S(2)}, u32[]{:S(2)}) collective-permute-start(f32[32]{0:T(128)S(1)} %get-tuple-element.72), channel_id=1, source_target_pairs={{0,8},{2,10},{4,12},{6,14},{8,16},{10,18},{12,20},{14,22},{16,24},... | collective-permute-start | bytes 392 | tf_op jit(solution)/shard_map/ppermute | solution.py:287
  76.3 1.3 collective-permute-start.9
  77.9 5.5 %collective-permute-start.7 = (f32[32,2048]{1,0:T(8,128)S(1)}, f32[32,2048]{1,0:T(8,128)S(1)}, u32[]{:S(2)}, u32[]{:S(2)}) collective-permute-start(f32[32,2048]{1,0:T(8,128)S(1)} %get-tuple-element.45), channel_id=1, source_target_pairs={{0,16},{2,18},{4,20},{6,22},{8,24},{10,26},{12,28},{14,30},{1,17},... | collective-permute-start | bytes 786440 | tf_op jit(solution)/shard_map/ppermute | solution.py:287
  83.4 7.0 %collective-permute-done.9 = f32[32,2048]{1,0:T(8,128)S(1)} collective-permute-done((f32[32,2048]{1,0:T(8,128)S(1)}, f32[32,2048]{1,0:T(8,128)S(1)}, u32[]{:S(2)}, u32[]{:S(2)}) %collective-permute-start.9) | collective-permute-done | bytes 262176 | tf_op jit(solution)/shard_map/ppermute | solution.py:287
  90.6 0.1 fusion.13
  90.7 0.1 fusion.5
  90.8 1.7 collective-permute-start.10
  92.6 1.9 copy.20
  94.5 0.7 copy.21
  95.2 1.9 copy.19
  97.1 0.7 broadcast_in_dim_reshape.2.skip_ref
  98.1 18.0 %shard_map.93.i_ref = bf16[1024,2048]{1,0:T(8,128)(2,1)} custom-call(bf16[1024,2048]{1,0:T(8,128)(2,1)} %convolution_convert_fusion.1.x_ref, bf16[1024,256]{1,0:T(8,128)(2,1)} %convolution_convert_fusion.2.b_ref.s_ref, f32[8,512,8]{2,1,0:T(8,128)} %bitcast.74, f32[8,8,512]{2,1,0:T(8,128)} %bitcast.82, f32[8,512,8]{2,1,0:T(8,128)} %bitcast.77, ...), custom_call_target="tpu_custom_call" | custom-call | tf_op jit(solution)/shard_map/pallas_call | solution.py:166
  116.1 1.4 maximum_select_fusion.1
  117.5 0.2 multiply_add_fusion.1
  117.8 0.2 fusion.2
  118.1 2.6 %collective-permute-done.11 = f32[2,64,2048]{2,1,0:T(8,128)S(1)} collective-permute-done((f32[2,64,2048]{2,1,0:T(8,128)S(1)}, f32[2,64,2048]{2,1,0:T(8,128)S(1)}, u32[]{:S(2)}, u32[]{:S(2)}) %collective-permute-start.11) | collective-permute-done | bytes 1048608 | tf_op jit(solution)/shard_map/ppermute | solution.py:308
  120.7 1.5 maximum_select_fusion.c_ref
  122.2 10.8 %shard_map.94.g_ref = bf16[1024,2048]{1,0:T(8,128)(2,1)} custom-call(bf16[1024,2048]{1,0:T(8,128)(2,1)} %shard_map.93.i_ref, bf16[1024,2048]{1,0:T(8,128)(2,1)} %convolution_convert_fusion.g_ref, bf16[1024,256]{1,0:T(8,128)(2,1)} %convolution_convert_fusion.2.b_ref.s_ref, f32[8,512,8]{2,1,0:T(8,128)} %bitcast.75, f32[2,128,2048]{2,1,0:T(8,128)} %maximum_select_fusion.c_ref), custom_call_target="tpu_custom_call" | custom-call | tf_op jit(solution)/shard_map/pallas_call | solution.py:203
  133.0 7.9 %shard_map.97 = f32[512,512]{1,0:T(8,128)} custom-call(s32[1]{0:T(128)} %bitcast.32.at_ref, bf16[1024,2048]{1,0:T(8,128)(2,1)} %shard_map.94.g_ref, bf16[2048,2048]{1,0:T(8,128)(2,1)} %v_ref.5, bf16[2048,2048]{1,0:T(8,128)(2,1)} %v_ref.5), custom_call_target="tpu_custom_call" | custom-call | tf_op jit(solution)/shard_map/pallas_call | solution.py:231
  140.9 1.5 collective-permute-start.13
  142.4 7.9 %shard_map.96 = f32[512,512]{1,0:T(8,128)} custom-call(s32[1]{0:T(128)} %bitcast.31.at_ref, bf16[1024,2048]{1,0:T(8,128)(2,1)} %shard_map.94.g_ref, bf16[2048,2048]{1,0:T(8,128)(2,1)} %v_ref.5, bf16[2048,2048]{1,0:T(8,128)(2,1)} %v_ref.5), custom_call_target="tpu_custom_call" | custom-call | tf_op jit(solution)/shard_map/pallas_call | solution.py:231
  150.4 0.5 collective-permute-start.12
  150.9 12.3 %shard_map.95 = f32[512,1024]{1,0:T(8,128)} custom-call(s32[1]{0:T(128)} %bitcast.at_ref, bf16[1024,2048]{1,0:T(8,128)(2,1)} %shard_map.94.g_ref, bf16[2048,2048]{1,0:T(8,128)(2,1)} %v_ref.5, bf16[2048,2048]{1,0:T(8,128)(2,1)} %v_ref.5), custom_call_target="tpu_custom_call" | custom-call | tf_op jit(solution)/shard_map/pallas_call | solution.py:231
  163.2 4.0 %collective-permute-done.13 = f32[512,512]{1,0:T(8,128)S(1)} collective-permute-done((f32[512,512]{1,0:T(8,128)}, f32[512,512]{1,0:T(8,128)S(1)}, u32[]{:S(2)}, u32[]{:S(2)}) %collective-permute-start.13) | collective-permute-done | bytes 1048608 | tf_op jit(solution)/shard_map/ppermute | solution.py:381
  167.2 21.6 %collective-permute-done.12 = f32[512,512]{1,0:T(8,128)S(1)} collective-permute-done((f32[512,512]{1,0:T(8,128)}, f32[512,512]{1,0:T(8,128)S(1)}, u32[]{:S(2)}, u32[]{:S(2)}) %collective-permute-start.12) | collective-permute-done | bytes 1048608 | tf_op jit(solution)/shard_map/ppermute | solution.py:381
  188.8 2.9 %fusion = bf16[512,1024]{1,0:T(8,128)(2,1)} fusion(f32[512,1024]{1,0:T(8,128)} %shard_map.95, f32[512,512]{1,0:T(8,128)S(1)} %collective-permute-done.13, f32[512,512]{1,0:T(8,128)S(1)} %collective-permute-done.12), kind=kLoop, calls=%fused_computation.4 | loop fusion | flops 1572864 | bytes 5242880 | tf_op jit(solution)/shard_map/convert_element_type | solution.py:386
  (89 shorter events, 2.8 us)
Async XLA Ops:
  0.0 25.1 %copy-start = (bf16[2048,256]{1,0:T(8,128)(2,1)S(1)}, bf16[2048,256]{1,0:T(8,128)(2,1)}, u32[]{:S(2)}) copy-start(bf16[2048,256]{1,0:T(8,128)(2,1)} %param.12) | copy-start | bytes 3145732
  0.0 4.5 %copy-start.13 = (f32[32]{0:T(128)S(1)}, f32[32]{0:T(128)}, u32[]{:S(2)}) copy-start(f32[32]{0:T(128)} %param.15) | copy-start | bytes 388
  0.0 4.5 %copy-start.10 = (bf16[2048,32]{0,1:T(8,128)(2,1)S(1)}, bf16[2048,32]{0,1:T(8,128)(2,1)}, u32[]{:S(2)}) copy-start(bf16[2048,32]{0,1:T(8,128)(2,1)} %param.13) | copy-start | bytes 393220
  0.0 4.5 %copy-start.11 = (f32[32]{0:T(128)S(1)}, f32[32]{0:T(128)}, u32[]{:S(2)}) copy-start(f32[32]{0:T(128)} %param.14) | copy-start | bytes 388
  9.2 86.0 %copy-start.9 = (f32[2,512,32]{1,2,0:T(8,128)}, f32[2,512,32]{1,2,0:T(8,128)S(1)}, u32[]{:S(2)}) copy-start(f32[2,512,32]{1,2,0:T(8,128)S(1)} %fusion.1) | copy-start | bytes 393220
  9.4 31.7 %collective-permute-start = (f32[2,32]{1,0:T(2,128)S(1)}, f32[2,32]{1,0:T(2,128)S(1)}, u32[]{:S(2)}, u32[]{:S(2)}) collective-permute-start(f32[2,32]{1,0:T(2,128)S(1)} %pad_maximum_fusion.9), channel_id=1, source_target_pairs={{0,2},{2,0},{4,6},{6,4},{8,10},{10,8},{12,14},{14,12},{16,18},{18,... | collective-permute-start | bytes 776 | tf_op jit(solution)/shard_map/ppermute | solution.py:275
  10.0 15.0 %copy-start.2 = (bf16[1024,2048]{1,0:T(8,128)(2,1)S(1)}, bf16[1024,2048]{1,0:T(8,128)(2,1)}, u32[]{:S(2)}) copy-start(bf16[1024,2048]{1,0:T(8,128)(2,1)} %shard_map.91) | copy-start | bytes 12582916
  39.1 6.9 %copy-start.4 = (f32[2,128,2048]{2,1,0:T(8,128)S(1)}, f32[2,128,2048]{2,1,0:T(8,128)}, u32[]{:S(2)}) copy-start(f32[2,128,2048]{2,1,0:T(8,128)} %shard_map.92) | copy-start | bytes 6291460
  41.0 5.0 %collective-permute-start.4 = (f32[2,64,2048]{2,1,0:T(8,128)S(1)}, f32[2,64,2048]{2,1,0:T(8,128)}, u32[]{:S(2)}, u32[]{:S(2)}) collective-permute-start(f32[2,64,2048]{2,1,0:T(8,128)S(1)} %slice_select_fusion), channel_id=1, source_target_pairs={{0,2},{2,0},{4,6},{6,4},{8,10},{10,8},{12,14},{14,12},{16,18},{18,... | collective-permute-start | bytes 3145736 | tf_op jit(solution)/shard_map/ppermute | solution.py:272
  41.1 4.6 %collective-permute-start.1 = (f32[2,32]{1,0:T(2,128)S(1)}, f32[2,32]{1,0:T(2,128)S(1)}, u32[]{:S(2)}, u32[]{:S(2)}) collective-permute-start(f32[2,32]{1,0:T(2,128)S(1)} %get-tuple-element.59), channel_id=1, source_target_pairs={{0,4},{2,6},{4,0},{6,2},{8,12},{10,14},{12,8},{14,10},{16,20},{18,... | collective-permute-start | bytes 776 | tf_op jit(solution)/shard_map/ppermute | solution.py:275
  47.5 1.0 copy-start.5
  47.5 1.3 copy-start.7
  47.5 3.5 %copy-start.3 = (bf16[1024,2048]{1,0:T(8,128)(2,1)S(1)}, bf16[1024,2048]{1,0:T(8,128)(2,1)}, u32[]{:S(2)}) copy-start(bf16[1024,2048]{1,0:T(8,128)(2,1)} %shard_map.91) | copy-start | bytes 12582916
  48.9 14.7 %collective-permute-start.5 = (f32[2,32,2048]{2,1,0:T(8,128)S(1)}, f32[2,32,2048]{2,1,0:T(8,128)S(1)}, u32[]{:S(2)}, u32[]{:S(2)}) collective-permute-start(f32[2,32,2048]{2,1,0:T(8,128)S(1)} %slice_select_fusion.2), channel_id=1, source_target_pairs={{0,4},{2,6},{4,0},{6,2},{8,12},{10,14},{12,8},{14,10},{16,20},{18,... | collective-permute-start | bytes 1572872 | tf_op jit(solution)/shard_map/ppermute | solution.py:272
  63.9 12.3 %collective-permute-start.8 = (f32[32,2048]{1,0:T(8,128)S(1)}, f32[32,2048]{1,0:T(8,128)S(1)}, u32[]{:S(2)}, u32[]{:S(2)}) collective-permute-start(f32[32,2048]{1,0:T(8,128)S(1)} %get-tuple-element.48), channel_id=1, source_target_pairs={{8,0},{10,2},{12,4},{14,6},{16,8},{18,10},{20,12},{22,14},{24,16},... | collective-permute-start | bytes 786440 | tf_op jit(solution)/shard_map/ppermute | solution.py:287
  65.2 11.0 %collective-permute-start.6 = (f32[32,2048]{1,0:T(8,128)S(1)}, f32[32,2048]{1,0:T(8,128)S(1)}, u32[]{:S(2)}, u32[]{:S(2)}) collective-permute-start(f32[32,2048]{1,0:T(8,128)S(1)} %get-tuple-element.47), channel_id=1, source_target_pairs={{0,8},{2,10},{4,12},{6,14},{8,16},{10,18},{12,20},{14,22},{16,24},... | collective-permute-start | bytes 786440 | tf_op jit(solution)/shard_map/ppermute | solution.py:287
  70.1 7.5 %collective-permute-start.3 = (f32[32]{0:T(128)S(1)}, f32[32]{0:T(128)S(1)}, u32[]{:S(2)}, u32[]{:S(2)}) collective-permute-start(f32[32]{0:T(128)S(1)} %get-tuple-element.73), channel_id=1, source_target_pairs={{8,0},{10,2},{12,4},{14,6},{16,8},{18,10},{20,12},{22,14},{24,16},... | collective-permute-start | bytes 392 | tf_op jit(solution)/shard_map/ppermute | solution.py:287
  71.4 6.2 %collective-permute-start.2 = (f32[32]{0:T(128)S(1)}, f32[32]{0:T(128)S(1)}, u32[]{:S(2)}, u32[]{:S(2)}) collective-permute-start(f32[32]{0:T(128)S(1)} %get-tuple-element.72), channel_id=1, source_target_pairs={{0,8},{2,10},{4,12},{6,14},{8,16},{10,18},{12,20},{14,22},{16,24},... | collective-permute-start | bytes 392 | tf_op jit(solution)/shard_map/ppermute | solution.py:287
  76.3 14.2 %collective-permute-start.9 = (f32[32,2048]{1,0:T(8,128)S(1)}, f32[32,2048]{1,0:T(8,128)S(1)}, u32[]{:S(2)}, u32[]{:S(2)}) collective-permute-start(f32[32,2048]{1,0:T(8,128)S(1)} %get-tuple-element.46), channel_id=1, source_target_pairs={{16,0},{18,2},{20,4},{22,6},{24,8},{26,10},{28,12},{30,14},{17,1},... | collective-permute-start | bytes 786440 | tf_op jit(solution)/shard_map/ppermute | solution.py:287
  77.9 12.6 %collective-permute-start.7 = (f32[32,2048]{1,0:T(8,128)S(1)}, f32[32,2048]{1,0:T(8,128)S(1)}, u32[]{:S(2)}, u32[]{:S(2)}) collective-permute-start(f32[32,2048]{1,0:T(8,128)S(1)} %get-tuple-element.45), channel_id=1, source_target_pairs={{0,16},{2,18},{4,20},{6,22},{8,24},{10,26},{12,28},{14,30},{1,17},... | collective-permute-start | bytes 786440 | tf_op jit(solution)/shard_map/ppermute | solution.py:287
  90.7 6.4 %copy-start.12 = (f32[32]{0:T(128)S(1)}, f32[32]{0:T(128)}, u32[]{:S(2)}) copy-start(f32[32]{0:T(128)} %param.16) | copy-start | bytes 388
  90.8 25.3 %collective-permute-start.10 = (f32[2,32,2048]{2,1,0:T(8,128)S(1)}, f32[2,32,2048]{2,1,0:T(8,128)}, u32[]{:S(2)}, u32[]{:S(2)}) collective-permute-start(f32[2,32,2048]{2,1,0:T(8,128)S(1)} %get-tuple-element.38), channel_id=1, source_target_pairs={{0,4},{2,6},{4,0},{6,2},{8,12},{10,14},{12,8},{14,10},{16,20},{18,... | collective-permute-start | bytes 1572872 | tf_op jit(solution)/shard_map/ppermute | solution.py:308
  98.1 19.4 %copy-start.6 = (f32[2,64,2048]{2,1,0:T(8,128)S(1)}, f32[2,64,2048]{2,1,0:T(8,128)}, u32[]{:S(2)}) copy-start(f32[2,64,2048]{2,1,0:T(8,128)} %copy-done.5) | copy-start | bytes 3145732
  98.1 19.4 %copy-start.8 = (f32[2,64,2048]{2,1,0:T(8,128)S(1)}, f32[2,64,2048]{2,1,0:T(8,128)}, u32[]{:S(2)}) copy-start(f32[2,64,2048]{2,1,0:T(8,128)} %copy-done.7) | copy-start | bytes 3145732
  118.0 2.7 %collective-permute-start.11 = (f32[2,64,2048]{2,1,0:T(8,128)S(1)}, f32[2,64,2048]{2,1,0:T(8,128)S(1)}, u32[]{:S(2)}, u32[]{:S(2)}) collective-permute-start(f32[2,64,2048]{2,1,0:T(8,128)S(1)} %get-tuple-element.20), channel_id=1, source_target_pairs={{0,2},{2,0},{4,6},{6,4},{8,10},{10,8},{12,14},{14,12},{16,18},{18,... | collective-permute-start | bytes 3145736 | tf_op jit(solution)/shard_map/ppermute | solution.py:308
  140.9 26.2 %collective-permute-start.13 = (f32[512,512]{1,0:T(8,128)}, f32[512,512]{1,0:T(8,128)S(1)}, u32[]{:S(2)}, u32[]{:S(2)}) collective-permute-start(f32[512,512]{1,0:T(8,128)} %shard_map.97), channel_id=1, source_target_pairs={{0,1},{1,0},{2,3},{3,2},{4,5},{5,4},{6,7},{7,6},{8,9},{9,8},{10,11... | collective-permute-start | bytes 3145736 | tf_op jit(solution)/shard_map/ppermute | solution.py:381
  150.4 38.5 %collective-permute-start.12 = (f32[512,512]{1,0:T(8,128)}, f32[512,512]{1,0:T(8,128)S(1)}, u32[]{:S(2)}, u32[]{:S(2)}) collective-permute-start(f32[512,512]{1,0:T(8,128)} %shard_map.96), channel_id=1, source_target_pairs={{0,1},{1,0},{2,3},{3,2},{4,5},{5,4},{6,7},{7,6},{8,9},{9,8},{10,11... | collective-permute-start | bytes 3145736 | tf_op jit(solution)/shard_map/ppermute | solution.py:381
  150.9 40.8 %copy-start.1 = (bf16[2048,256]{1,0:T(8,128)(2,1)S(1)}, bf16[2048,256]{1,0:T(8,128)(2,1)}, u32[]{:S(2)}) copy-start(bf16[2048,256]{1,0:T(8,128)(2,1)} %param.12) | copy-start | bytes 3145732
